TPU v7x, 32 devices: a whole 2x2x4 slice. The times are simulated.
32 devices in a mesh: rows: 16 (over z, y, core), cols: 2 (over x).
Axes of the slice: x: 2, y: 2, z: 4, core: 2. Of those that a mesh axis runs over, the one named last changes fastest.
Arguments:
- design: bfloat16 [32768, 6144], P('rows', 'cols'), may hold values from -0.03125 to 0.03125
- targets: bfloat16 [32768, 128], P('rows'), may hold values from -6 to 6
- col_scale: float32 [6144], P('cols'), may hold values from 0.1 to 1
Outputs:
- solution: float32 [6144, 128], P('cols', 'rows')
- residual: float32 [32768, 128], P('rows')
All inputs are finite; a program needn't handle non-finite values.
Results may differ from a plain program's by a relative error of at most 0.0065.
Values may be sent and summed in bfloat16 or wider, within the bound.
A program may use at most 128 MiB of HBM per device.

v0:
```python
import jax
import jax.numpy as jnp
from jax import lax
from jax.sharding import PartitionSpec as P

ITERS = 6


def local_back(design, vectors):
    return lax.dot_general(
        design, vectors, (((0,), (0,)), ((), ())), preferred_element_type=jnp.float32
    )


def per_device(design, targets, col_scale):
    fits = targets.shape[1]
    row_count = lax.axis_size("rows")
    residual = targets.astype(jnp.float32)
    scale = col_scale[:, None]

    def gradient_of(vectors):
        return scale * lax.psum(local_back(design, vectors), "rows")

    def squared(values):
        return lax.psum(jnp.sum(values * values, axis=0), "cols")

    gradient = gradient_of(targets)
    gamma = squared(gradient)
    solution = jnp.zeros(gradient.shape, jnp.float32)
    direction = gradient
    for step in range(ITERS):
        scaled_dir = (scale * direction).astype(jnp.bfloat16)
        image = lax.psum(
            jnp.dot(design, scaled_dir, preferred_element_type=jnp.float32).astype(jnp.bfloat16),
            "cols",
        ).astype(jnp.float32)
        delta = lax.psum(jnp.sum(image * image, axis=0), "rows")
        alpha = gamma / delta
        solution = solution + alpha * direction
        residual = residual - alpha * image
        if step + 1 < ITERS:
            gradient = gradient_of(residual.astype(jnp.bfloat16))
            gamma_new = squared(gradient)
            direction = gradient + gamma_new / gamma * direction
            gamma = gamma_new
    own = fits // row_count
    solution_part = lax.dynamic_slice_in_dim(solution, lax.axis_index("rows") * own, own, 1)
    return (solution_part, residual)


def solution(mesh):
    in_specs = (P("rows", "cols"), P("rows", None), P("cols"))
    out_specs = (P("cols", "rows"), P("rows", None))
    return jax.shard_map(
        per_device, mesh=mesh, in_specs=in_specs, out_specs=out_specs, check_vma=False
    )
```

profile of v0, /device:TPU:0, one launch (start us, length us, event | category | flops | bytes accessed | tf_op | source)
XLA Modules:
  0.0 1142.6 jit_solution(10677562298321157389)
XLA Ops:
  16.5 98.8 %all-reduce.13.cloned.1.call-done = f32[3072,128]{1,0:T(8,128)} async-done(((f32[3072,128]{1,0:T(8,128)}), f32[3072,128]{1,0:T(8,128)}) %all-reduce.13.cloned.1.call-update) | async-done | bytes 1572880 | tf_op jit(solution)/shard_map/psum | solution.py:22
  117.2 10.4 fusion
  132.8 22.5 %all-reduce.15.cloned.1.call-done = bf16[2048,128]{0,1:T(8,128)(2,1)} async-done(((bf16[2048,128]{0,1:T(8,128)(2,1)}), bf16[2048,128]{0,1:T(8,128)(2,1)}) %all-reduce.15.cloned.1.call-update) | async-done | bytes 524304 | tf_op jit(solution)/shard_map/psum | solution.py:33
  156.5 33.2 %psum.171 = f32[128]{0:T(128)S(1)} all-reduce(f32[128]{0:T(128)S(1)} %fusion.11), channel_id=1, replica_groups=mesh['rows'=16,'cols'=2] {'rows'}, use_global_device_ids=true, to_apply=%region_5.0 | all-reduce | flops 128 | bytes 1024 | tf_op jit(solution)/shard_map/psum | solution.py:37
  189.8 11.0 convolution_bitcast_fusion.4
  200.8 92.3 %all-reduce.17.cloned.1.call-done = f32[3072,128]{1,0:T(8,128)} async-done(((f32[3072,128]{1,0:T(8,128)}), f32[3072,128]{1,0:T(8,128)}) %all-reduce.17.cloned.1.call-update) | async-done | bytes 1572880 | tf_op jit(solution)/shard_map/psum | solution.py:22
  312.2 27.6 %all-reduce.19.cloned.1.call-done = bf16[2048,128]{0,1:T(8,128)(2,1)} async-done(((bf16[2048,128]{0,1:T(8,128)(2,1)}), bf16[2048,128]{0,1:T(8,128)(2,1)}) %all-reduce.19.cloned.1.call-update) | async-done | bytes 524304 | tf_op jit(solution)/shard_map/psum | solution.py:33
  341.1 33.4 %psum.175 = f32[128]{0:T(128)S(1)} all-reduce(f32[128]{0:T(128)S(1)} %fusion.13), channel_id=1, replica_groups=mesh['rows'=16,'cols'=2] {'rows'}, use_global_device_ids=true, to_apply=%region_11.0 | all-reduce | flops 128 | bytes 1024 | tf_op jit(solution)/shard_map/psum | solution.py:37
  374.5 11.3 convolution_bitcast_fusion.3
  385.9 92.3 %all-reduce.21.cloned.1.call-done = f32[3072,128]{1,0:T(8,128)} async-done(((f32[3072,128]{1,0:T(8,128)}), f32[3072,128]{1,0:T(8,128)}) %all-reduce.21.cloned.1.call-update) | async-done | bytes 1572880 | tf_op jit(solution)/shard_map/psum | solution.py:22
  498.5 27.6 %all-reduce.23.cloned.1.call-done = bf16[2048,128]{0,1:T(8,128)(2,1)} async-done(((bf16[2048,128]{0,1:T(8,128)(2,1)}), bf16[2048,128]{0,1:T(8,128)(2,1)}) %all-reduce.23.cloned.1.call-update) | async-done | bytes 524304 | tf_op jit(solution)/shard_map/psum | solution.py:33
  527.4 33.2 %psum.179 = f32[128]{0:T(128)S(1)} all-reduce(f32[128]{0:T(128)S(1)} %fusion.15), channel_id=1, replica_groups=mesh['rows'=16,'cols'=2] {'rows'}, use_global_device_ids=true, to_apply=%region_17.0 | all-reduce | flops 128 | bytes 1024 | tf_op jit(solution)/shard_map/psum | solution.py:37
  560.6 11.5 %convolution_bitcast_fusion.2 = f32[3072,128]{1,0:T(8,128)} fusion(bf16[2048,3072]{1,0:T(8,128)(2,1)} %param.3, bf16[2048,128]{0,1:T(8,128)(2,1)} %all-reduce.23.cloned.1.call-done, f32[128]{0:T(128)S(1)} %div.37, bf16[2048,128]{0,1:T(8,128)(2,1)} %all-reduce.19.cloned.1.call-done, bf16[2048,128]{0,1:T(8,128)(2,1)} %all-reduce.15.cloned.1.call-done, ...), kind=kOutput, calls=%fused_computation.2 | convolution fusion | flops 1613496320 | bytes 16254464 | tf_op jit(solution)/shard_map/dot_general | solution.py:10
  572.2 92.0 %all-reduce.25.cloned.1.call-done = f32[3072,128]{1,0:T(8,128)} async-done(((f32[3072,128]{1,0:T(8,128)}), f32[3072,128]{1,0:T(8,128)}) %all-reduce.25.cloned.1.call-update) | async-done | bytes 1572880 | tf_op jit(solution)/shard_map/psum | solution.py:22
  684.9 27.6 %all-reduce.27.cloned.1.call-done = bf16[2048,128]{0,1:T(8,128)(2,1)} async-done(((bf16[2048,128]{0,1:T(8,128)(2,1)}), bf16[2048,128]{0,1:T(8,128)(2,1)}) %all-reduce.27.cloned.1.call-update) | async-done | bytes 524304 | tf_op jit(solution)/shard_map/psum | solution.py:33
  713.8 33.2 %psum.183 = f32[128]{0:T(128)S(1)} all-reduce(f32[128]{0:T(128)S(1)} %fusion.17), channel_id=1, replica_groups=mesh['rows'=16,'cols'=2] {'rows'}, use_global_device_ids=true, to_apply=%region_23.0 | all-reduce | flops 128 | bytes 1024 | tf_op jit(solution)/shard_map/psum | solution.py:37
  759.4 92.2 %all-reduce.29.cloned.1.call-done = f32[3072,128]{1,0:T(8,128)} async-done(((f32[3072,128]{1,0:T(8,128)}), f32[3072,128]{1,0:T(8,128)}) %all-reduce.29.cloned.1.call-update) | async-done | bytes 1572880 | tf_op jit(solution)/shard_map/psum | solution.py:22
  861.9 10.3 fusion.4
  872.3 27.6 %all-reduce.31.cloned.1.call-done = bf16[2048,128]{0,1:T(8,128)(2,1)} async-done(((bf16[2048,128]{0,1:T(8,128)(2,1)}), bf16[2048,128]{0,1:T(8,128)(2,1)}) %all-reduce.31.cloned.1.call-update) | async-done | bytes 524304 | tf_op jit(solution)/shard_map/psum | solution.py:33
  901.2 33.3 %psum.187 = f32[128]{0:T(128)S(1)} all-reduce(f32[128]{0:T(128)S(1)} %fusion.19), channel_id=1, replica_groups=mesh['rows'=16,'cols'=2] {'rows'}, use_global_device_ids=true, to_apply=%region_29.0 | all-reduce | flops 128 | bytes 1024 | tf_op jit(solution)/shard_map/psum | solution.py:37
  934.5 11.3 convolution_bitcast_fusion
  945.8 92.0 %all-reduce.33.cloned.1.call-done = f32[3072,128]{1,0:T(8,128)} async-done(((f32[3072,128]{1,0:T(8,128)}), f32[3072,128]{1,0:T(8,128)}) %all-reduce.33.cloned.1.call-update) | async-done | bytes 1572880 | tf_op jit(solution)/shard_map/psum | solution.py:22
  1058.9 27.3 %all-reduce.35.cloned.1.call-done = bf16[2048,128]{0,1:T(8,128)(2,1)} async-done(((bf16[2048,128]{0,1:T(8,128)(2,1)}), bf16[2048,128]{0,1:T(8,128)(2,1)}) %all-reduce.35.cloned.1.call-update) | async-done | bytes 524304 | tf_op jit(solution)/shard_map/psum | solution.py:33
  1087.5 33.3 %psum.191 = f32[128]{0:T(128)S(1)} all-reduce(f32[128]{0:T(128)S(1)} %fusion.21), channel_id=1, replica_groups=mesh['rows'=16,'cols'=2] {'rows'}, use_global_device_ids=true, to_apply=%region_35.0 | all-reduce | flops 128 | bytes 1024 | tf_op jit(solution)/shard_map/psum | solution.py:37
  (92 shorter events, 142.3 us)
Async XLA Ops:
  7.2 108.2 %all-reduce.13.cloned.1.call-start = ((), (), s32[]{:S(2)}) async-start(), calls=%async_computation | async-start | bytes 3145728 | tf_op jit(solution)/shard_map/psum | solution.py:22
  16.5 98.9 %copy-start.6 = (f32[3072]{0:T(1024)S(1)}, f32[3072]{0:T(1024)}, u32[]{:S(2)}) copy-start(f32[3072]{0:T(1024)} %param.5) | copy-start | bytes 36868
  16.5 138.8 %all-reduce.15.cloned.1.call-start = ((), (), s32[]{:S(2)}) async-start(), calls=%async_computation.1 | async-start | bytes 1048576 | tf_op jit(solution)/shard_map/psum | solution.py:33
  117.2 10.4 copy-start.7
  127.6 165.5 %all-reduce.17.cloned.1.call-start = ((), (), s32[]{:S(2)}) async-start(), calls=%async_computation.2 | async-start | bytes 3145728 | tf_op jit(solution)/shard_map/psum | solution.py:22
  127.9 72.8 %copy-start.5 = (bf16[2048,128]{0,1:T(8,128)(2,1)}, bf16[2048,128]{0,1:T(8,128)(2,1)S(1)}, u32[]{:S(2)}) copy-start(bf16[2048,128]{0,1:T(8,128)(2,1)S(1)} %copy.5) | copy-start | bytes 1572868
  200.7 139.1 %all-reduce.19.cloned.1.call-start = ((), (), s32[]{:S(2)}) async-start(), calls=%async_computation.3 | async-start | bytes 1048576 | tf_op jit(solution)/shard_map/psum | solution.py:33
  312.2 166.1 %all-reduce.21.cloned.1.call-start = ((), (), s32[]{:S(2)}) async-start(), calls=%async_computation.4 | async-start | bytes 3145728 | tf_op jit(solution)/shard_map/psum | solution.py:22
  385.9 140.3 %all-reduce.23.cloned.1.call-start = ((), (), s32[]{:S(2)}) async-start(), calls=%async_computation.5 | async-start | bytes 1048576 | tf_op jit(solution)/shard_map/psum | solution.py:33
  487.0 1.2 copy-start
  498.5 165.7 %all-reduce.25.cloned.1.call-start = ((), (), s32[]{:S(2)}) async-start(), calls=%async_computation.6 | async-start | bytes 3145728 | tf_op jit(solution)/shard_map/psum | solution.py:22
  572.1 140.4 %all-reduce.27.cloned.1.call-start = ((), (), s32[]{:S(2)}) async-start(), calls=%async_computation.7 | async-start | bytes 1048576 | tf_op jit(solution)/shard_map/psum | solution.py:33
  673.4 1.1 copy-start.1
  684.9 166.7 %all-reduce.29.cloned.1.call-start = ((), (), s32[]{:S(2)}) async-start(), calls=%async_computation.8 | async-start | bytes 3145728 | tf_op jit(solution)/shard_map/psum | solution.py:22
  749.3 1.0 copy-start.3
  759.4 140.6 %all-reduce.31.cloned.1.call-start = ((), (), s32[]{:S(2)}) async-start(), calls=%async_computation.9 | async-start | bytes 1048576 | tf_op jit(solution)/shard_map/psum | solution.py:33
  860.8 1.1 copy-start.2
  872.3 165.6 %all-reduce.33.cloned.1.call-start = ((), (), s32[]{:S(2)}) async-start(), calls=%async_computation.10 | async-start | bytes 3145728 | tf_op jit(solution)/shard_map/psum | solution.py:22
  945.7 140.5 %all-reduce.35.cloned.1.call-start = ((), (), s32[]{:S(2)}) async-start(), calls=%async_computation.11 | async-start | bytes 1048576 | tf_op jit(solution)/shard_map/psum | solution.py:33
  1047.0 1.2 copy-start.4
Sparse Core Ops, SparseCore 0:
  16.6 98.6 all-reduce.12
  127.7 27.5 all-reduce.14
  200.9 92.2 all-reduce.16
  312.3 27.5 all-reduce.18
  386.0 92.2 all-reduce.20
  498.6 27.5 all-reduce.22
  572.2 91.9 all-reduce.24
  685.0 27.5 all-reduce.26
  759.5 92.0 all-reduce.28
  872.4 27.5 all-reduce.30
  945.9 91.9 all-reduce.32
  1058.7 27.5 all-reduce.34
where the time goes:
time: 1150 us; the launch traced here: 1140 us
  waiting for transfers between devices  720 us (63%)
  blocking collectives  229 us (20%)
  matrix products  125 us (11%)
  other arithmetic  41.2 us (4%)
  between operations  14.8 us (1%)
    psum x6, waiting for transfers between devices, gradient_of(): return scale * lax.psum(local_back(design, vectors), 'rows')  560 us
    psum x6, blocking collectives, per_device(): delta = lax.psum(jnp.sum(image * image, axis=0), 'rows')  200 us
    psum x6, waiting for transfers between devices, per_device(): lax.psum(jnp.dot(design, scaled_dir, preferred_element_type=jnp.float32)....  160 us
    dot_general x6, matrix products, local_back(): lax.dot_general(design, vectors, (((0,), (0,)), ((), ())), preferred_elem...  63.3 us
    dot_general x6, matrix products, per_device(): jnp.dot(design, scaled_dir, preferred_element_type=jnp.float32)  61.9 us
    psum x6, blocking collectives, squared(): return lax.psum(jnp.sum(values * values, axis=0), 'cols')  29.6 us
  transfers between devices with their start and end apart: 12, of which 12 were waited for; matrix products, arithmetic and copies ran while one was open for 0% of the time, Pallas kernels for 0%

commit v1 on v0

v1 whole, which is shorter than its diff:
```python
import functools

import jax
import jax.numpy as jnp
from jax import lax
from jax.experimental import pallas as pl
from jax.experimental.pallas import tpu as pltpu
from jax.sharding import PartitionSpec as P

ITERS = 6
BLOCKS = 4
F32 = jnp.float32
BF16 = jnp.bfloat16
MESH = pl.DeviceIdType.MESH


def kernel(n, design_hbm, targets_ref, scale_ref, sol_ref, res_ref,
           design, h_ref, img, spm, sp_all, xs, xr, cs, cr, rs, rr, st, gx,
           g_ref, p_ref, gam_ref,
           load_sem, x_send, x_recv, c_send, c_recv, r_send, r_recv,
           a_send, a_recv, f_send, s_send, s_recv, g_send, g_recv):
    rows, width = design.shape
    fits = targets_ref.shape[1]
    own = fits // n
    chips = n // 2
    block = rows // BLOCKS
    wide = 512 if width % 512 == 0 else width
    r, c = lax.axis_index("rows"), lax.axis_index("cols")
    core, chip = lax.rem(r, 2), lax.div(r, 2)
    sibling = r + 1 - 2 * core
    partner = (r, 1 - c)

    def remote(src, dst, send, recv, to):
        return pltpu.make_async_remote_copy(
            src_ref=src, dst_ref=dst, send_sem=send, recv_sem=recv,
            device_id=to, device_id_type=MESH)

    def load(b):
        at = pl.ds(b * block, block)
        return pltpu.make_async_copy(design_hbm.at[at], design.at[at], load_sem.at[b])

    for b in range(BLOCKS):
        load(b).start()
    barrier = pltpu.get_barrier_semaphore()

    @pl.loop(1, n)
    def _(d):
        pl.semaphore_signal(barrier, inc=1, device_id=(lax.rem(r + d, n), c), device_id_type=MESH)

    pl.semaphore_signal(barrier, inc=1, device_id=partner, device_id_type=MESH)

    lane = lax.broadcasted_iota(jnp.int32, (own, fits), 1)
    row = lax.broadcasted_iota(jnp.int32, (own, fits), 0)
    mine = (lane == row + own * r).astype(F32)

    def rows_of(b):
        return pl.ds(pl.multiple_of(b * block, block), block)

    def back_block(b, vectors):
        left = jnp.transpose(vectors).astype(BF16)
        at = rows_of(b)

        @pl.loop(0, width // wide)
        def _(j):
            cols = pl.ds(pl.multiple_of(j * wide, wide), wide)
            h_ref[:, cols] += jnp.dot(left, design[at, cols], preferred_element_type=F32)

    def reduce_scatter():
        def fits_of(i):
            return pl.ds(pl.multiple_of(i * own, own), own)

        for j in range(chips):
            cs[j] = h_ref[fits_of(2 * j + 1 - core), :].astype(BF16)
        swap = remote(cs, cr, c_send, c_recv, (sibling, c))
        swap.start()
        swap.wait()

        def send(d):
            to = lax.rem(chip + d, chips)
            return remote(rs.at[to], rr.at[chip], r_send.at[to], r_recv.at[chip], (2 * to + core, c))

        def arrived(d):
            frm = lax.rem(chip + d, chips)
            return remote(rs.at[frm], rr.at[frm], r_send.at[frm], r_recv.at[frm], (2 * frm + core, c))

        @pl.loop(1, chips)
        def _(d):
            to = lax.rem(chip + d, chips)
            rs[to] = (h_ref[fits_of(2 * to + core), :] + cr[to].astype(F32)).astype(BF16)
            send(d).start()

        h_ref[fits_of(r), :] += cr[chip].astype(F32)

        @pl.loop(1, chips)
        def _(d):
            arrived(d).wait_recv()
            h_ref[fits_of(r), :] += rr[lax.rem(chip + d, chips)].astype(F32)

        @pl.loop(1, chips)
        def _(d):
            send(d).wait_send()

        return scale_ref[...] * h_ref[fits_of(r), :]

    def squared(g):
        gx[0] = jnp.broadcast_to(jnp.sum(g * g, axis=1, keepdims=True), (own, fits))
        swap = remote(gx.at[0], gx.at[1], g_send, g_recv, partner)
        swap.start()
        swap.wait()
        return gx[0] + gx[1]

    def gather():
        def send(d):
            to = lax.rem(chip + d, chips)
            return remote(sp_all.at[r], sp_all.at[r], a_send.at[to], a_recv.at[r], (2 * to + core, c))

        def relay(d):
            slot = 2 * lax.rem(chip + d, chips) + core
            return remote(sp_all.at[slot], sp_all.at[slot], f_send.at[lax.div(slot, 2)],
                          a_recv.at[slot], (sibling, c))

        def arrived(slot):
            return remote(sp_all.at[slot], sp_all.at[slot], a_send.at[0], a_recv.at[slot], (sibling, c))

        @pl.loop(1, chips)
        def _(d):
            send(d).start()

        relay(0).start()

        @pl.loop(1, chips)
        def _(d):
            arrived(2 * lax.rem(chip + d, chips) + core).wait_recv()
            relay(d).start()

        @pl.loop(0, chips)
        def _(d):
            arrived(2 * lax.rem(chip + d, chips) + 1 - core).wait_recv()

        for j in range(chips):
            pair = jnp.concatenate([sp_all[2 * j].astype(F32), sp_all[2 * j + 1].astype(F32)], axis=0)
            spm[2 * own * j:2 * own * (j + 1), :] = pair.astype(BF16)

        @pl.loop(1, chips)
        def _(d):
            send(d).wait_send()

        @pl.loop(0, chips)
        def _(d):
            relay(d).wait_send()

    def x_copy(b):
        return remote(xs.at[b], xr.at[b], x_send.at[b], x_recv.at[b], partner)

    def forward():
        @pl.loop(0, BLOCKS)
        def _(b):
            part = lax.dot_general(design[rows_of(b), :], spm[...], (((1,), (1,)), ((), ())),
                                   preferred_element_type=F32)
            xs[b] = part.astype(BF16)
            x_copy(b).start()

    def image_block(b, delta):
        x_copy(b).wait_recv()
        image = xs[b].astype(F32) + xr[b].astype(F32)
        img[rows_of(b), :] = image
        return image, delta + jnp.sum(image * image, axis=0, keepdims=True)

    def stat_send(d):
        to = lax.rem(r + d, n)
        return remote(st.at[r], st.at[r], s_send.at[to], s_recv.at[r], (to, c))

    def stats_start(delta):
        st[r] = jnp.concatenate(
            [delta, jnp.sum(gam_ref[...] * mine, axis=0, keepdims=True)], axis=0)

        @pl.loop(1, n)
        def _(d):
            stat_send(d).start()

    def stats_finish():
        @pl.loop(1, n)
        def _(d):
            frm = lax.rem(r + d, n)
            remote(st.at[frm], st.at[frm], s_send.at[frm], s_recv.at[frm], (frm, c)).wait_recv()

        @pl.loop(1, n)
        def _(d):
            stat_send(d).wait_send()

        total = st[0]
        for i in range(1, n):
            total = total + st[i]
        return total[1:2, :] / total[0:1, :]

    def x_done():
        @pl.loop(0, BLOCKS)
        def _(b):
            x_copy(b).wait_send()

    def own_fits(values):
        return jnp.sum(mine * values, axis=1, keepdims=True)

    def publish():
        sp_all[r] = (scale_ref[...] * p_ref[...]).astype(BF16)

    h_ref[...] = jnp.zeros_like(h_ref)
    res_ref[...] = targets_ref[...].astype(F32)
    sol_ref[...] = jnp.zeros_like(sol_ref)
    for b in range(BLOCKS):
        load(b).wait()

    @pl.loop(0, BLOCKS)
    def _(b):
        back_block(b, res_ref[rows_of(b), :])

    pl.semaphore_wait(barrier, n)
    g = reduce_scatter()
    g_ref[...] = g
    p_ref[...] = g
    publish()
    gam_ref[...] = squared(g)

    @pl.loop(0, ITERS - 1)
    def _(step):
        gather()
        forward()
        h_ref[...] = jnp.zeros_like(h_ref)

        def one(b, delta):
            image, delta = image_block(b, delta)
            back_block(b, image)
            return delta

        delta = lax.fori_loop(0, BLOCKS, one, jnp.zeros((1, fits), F32))
        stats_start(delta)
        h = reduce_scatter()
        alpha = stats_finish()
        own_alpha = own_fits(alpha)
        p = p_ref[...]
        sol_ref[...] += own_alpha * p
        g = g_ref[...] - own_alpha * h
        g_ref[...] = g
        gamma_new = squared(g)
        beta = (gamma_new / gam_ref[...])[:, 0:1]
        gam_ref[...] = gamma_new
        p_ref[...] = g + beta * p
        publish()
        x_done()
        res_ref[...] -= alpha * img[...]

    gather()
    forward()
    delta = lax.fori_loop(0, BLOCKS, lambda b, d: image_block(b, d)[1], jnp.zeros((1, fits), F32))
    stats_start(delta)
    alpha = stats_finish()
    sol_ref[...] += own_fits(alpha) * p_ref[...]
    res_ref[...] -= alpha * img[...]
    x_done()


def fused(n, design, targets, col_scale):
    rows, width = design.shape
    fits = targets.shape[1]
    own, chips, block = fits // n, n // 2, rows // BLOCKS
    vmem = pl.BlockSpec(memory_space=pltpu.VMEM)
    dma = pltpu.SemaphoreType.DMA
    sol, res = pl.pallas_call(
        functools.partial(kernel, n),
        out_shape=(jax.ShapeDtypeStruct((own, width), F32),
                   jax.ShapeDtypeStruct((rows, fits), F32)),
        in_specs=[pl.BlockSpec(memory_space=pl.ANY), vmem, vmem],
        out_specs=(vmem, vmem),
        scratch_shapes=[
            pltpu.VMEM((rows, width), BF16),
            pltpu.VMEM((fits, width), F32),
            pltpu.VMEM((rows, fits), F32),
            pltpu.VMEM((fits, width), BF16),
            pltpu.VMEM((n, own, width), BF16),
            pltpu.VMEM((BLOCKS, block, fits), BF16),
            pltpu.VMEM((BLOCKS, block, fits), BF16),
            pltpu.VMEM((chips, own, width), BF16),
            pltpu.VMEM((chips, own, width), BF16),
            pltpu.VMEM((chips, own, width), BF16),
            pltpu.VMEM((chips, own, width), BF16),
            pltpu.VMEM((n, 2, fits), F32),
            pltpu.VMEM((2, own, fits), F32),
            pltpu.VMEM((own, width), F32),
            pltpu.VMEM((own, width), F32),
            pltpu.VMEM((own, fits), F32),
            dma((BLOCKS,)), dma((BLOCKS,)), dma((BLOCKS,)), dma, dma,
            dma((chips,)), dma((chips,)), dma((chips,)), dma((n,)), dma((chips,)),
            dma((n,)), dma((n,)), dma, dma,
        ],
        compiler_params=pltpu.CompilerParams(
            collective_id=0, has_side_effects=True, vmem_limit_bytes=48 * 1024 * 1024),
        name="cg",
    )(design, targets, col_scale[None, :])
    return sol.T, res


def plain(design, targets, col_scale):
    fits = targets.shape[1]
    row_count = lax.axis_size("rows")
    residual = targets.astype(F32)
    scale = col_scale[:, None]

    def gradient_of(vectors):
        local = lax.dot_general(design, vectors, (((0,), (0,)), ((), ())), preferred_element_type=F32)
        return scale * lax.psum(local, "rows")

    def squared(values):
        return lax.psum(jnp.sum(values * values, axis=0), "cols")

    gradient = gradient_of(targets)
    gamma = squared(gradient)
    solution = jnp.zeros(gradient.shape, F32)
    direction = gradient
    for step in range(ITERS):
        scaled_dir = (scale * direction).astype(BF16)
        image = lax.psum(
            jnp.dot(design, scaled_dir, preferred_element_type=F32).astype(BF16), "cols"
        ).astype(F32)
        delta = lax.psum(jnp.sum(image * image, axis=0), "rows")
        alpha = gamma / delta
        solution = solution + alpha * direction
        residual = residual - alpha * image
        if step + 1 < ITERS:
            gradient = gradient_of(residual.astype(BF16))
            gamma_new = squared(gradient)
            direction = gradient + gamma_new / gamma * direction
            gamma = gamma_new
    own = fits // row_count
    part = lax.dynamic_slice_in_dim(solution, lax.axis_index("rows") * own, own, 1)
    return (part, residual)


def solution(mesh):
    n, pair = mesh.shape["rows"], mesh.shape["cols"]

    def per_device(design, targets, col_scale):
        rows, width = design.shape
        fits = targets.shape[1]
        fits_tile = fits % (8 * n) == 0 and fits % 128 == 0
        if pair == 2 and n % 2 == 0 and fits_tile and rows % (BLOCKS * 128) == 0 and width % 128 == 0:
            return fused(n, design, targets, col_scale)
        return plain(design, targets, col_scale)

    in_specs = (P("rows", "cols"), P("rows", None), P("cols"))
    out_specs = (P("cols", "rows"), P("rows", None))
    return jax.shard_map(
        per_device, mesh=mesh, in_specs=in_specs, out_specs=out_specs, check_vma=False
    )
```

time: 1150 us -> 271 us (0.24)
  waiting for transfers between devices: 720 us -> 0 us
  Pallas kernels: 0 us -> 267 us
  blocking collectives: 229 us -> 0 us
  matrix products: 125 us -> 0 us
  other arithmetic: 41.2 us -> 0 us
  between operations: 14.8 us -> 0.65 us
    psum x12 -> x0, waiting for transfers between devices: 720 us -> none  [the longest x6 560 us: gradient_of(): return scale * lax.psum(local_back(design, vectors), 'rows')]
    pallas_call x0 -> x1, Pallas kernels: none -> 267 us  [fused(): pl.pallas_call(functools.partial(kernel, n), out_shape=(jax.ShapeDtypeStr...]
    psum x12 -> x0, blocking collectives: 229 us -> none  [the longest x6 200 us: per_device(): delta = lax.psum(jnp.sum(image * image, axis=0), 'rows')]
    dot_general x12 -> x0, matrix products: 125 us -> none  [the longest x6 63.3 us: local_back(): lax.dot_general(design, vectors, (((0,), (0,)), ((), ())), preferred_elem...]
    reduce_sum x12 -> x0, other arithmetic: 18.7 us -> none  [the longest x6 11.3 us: squared(): return lax.psum(jnp.sum(values * values, axis=0), 'cols')]
    add x6 -> x0, other arithmetic: 17.3 us -> none  [the longest x5 10.8 us: per_device(): direction = gradient + gamma_new / gamma * direction]
  transfers between devices with their start and end apart: 12 -> 0, of which waited for: 12 -> 0; matrix products, arithmetic and copies ran while one was open for 0% -> 0% of each run, Pallas kernels for 0% -> 0%
where the time goes in v1:
time: 271 us
  Pallas kernels  267 us (99%)
  local copies, waits for them, and re-layouts  3.35 us (1%)
    pallas_call x1, Pallas kernels, fused(): pl.pallas_call(functools.partial(kernel, n), out_shape=(jax.ShapeDtypeStr...  267 us

profile of v1, /device:TPU:0, one launch (start us, length us, event | category | flops | bytes accessed | tf_op | source)
XLA Modules:
  0.0 270.6 jit_solution(5367002383160390190)
XLA Ops:
  0.6 0.0 copy-start
  0.6 1.0 copy-done
  1.7 0.0 copy-start.1
  1.7 0.7 copy-done.1
  2.4 266.6 %cg.1 = (f32[8,3072]{1,0:T(8,128)S(1)}, f32[2048,128]{1,0:T(8,128)S(1)}) custom-call(bf16[2048,3072]{1,0:T(8,128)(2,1)} %design_hbm.1, bf16[2048,128]{1,0:T(8,128)(2,1)S(1)} %copy-done, f32[1,3072]{1,0:T(1,128)S(1)} %bitcast.3), custom_call_target="tpu_custom_call" | custom-call | tf_op jit(solution)/shard_map/cg/pallas_call | solution.py:268
  269.0 0.6 copy.7
  269.7 1.0 copy.8
Async XLA Ops:
  0.6 1.0 copy-start
  1.7 0.7 copy-start.1

commit v2 on v1

--- a/solution.py
+++ b/solution.py
@@ -15,10 +15,10 @@
 
 
 def kernel(n, design_hbm, targets_ref, scale_ref, sol_ref, res_ref,
-           design, h_ref, img, spm, sp_all, xs, xr, cs, cr, rs, rr, st, gx,
+           design, h_ref, img, spm, sp_all, xs, xr, cs, cr, ys, yr, rs, rr, st, gx,
            g_ref, p_ref, gam_ref,
            load_sem, x_send, x_recv, c_send, c_recv, r_send, r_recv,
-           a_send, a_recv, f_send, s_send, s_recv, g_send, g_recv):
+           a_send, a_recv, b_send, f_send, y_send, y_recv, s_send, s_recv, g_send, g_recv):
     rows, width = design.shape
     fits = targets_ref.shape[1]
     own = fits // n
@@ -29,14 +29,23 @@
     core, chip = lax.rem(r, 2), lax.div(r, 2)
     sibling = r + 1 - 2 * core
     partner = (r, 1 - c)
+    side, place, line = lax.rem(chip, 2), lax.div(chip, 2), chips // 2
+    across = (r + 2 - 4 * side, c)
+    order = sorted(range(1, line), key=lambda d: -min(d, line - d))
+
+    def place_at(d):
+        return lax.rem(place + d, line)
 
     def remote(src, dst, send, recv, to):
         return pltpu.make_async_remote_copy(
             src_ref=src, dst_ref=dst, send_sem=send, recv_sem=recv,
             device_id=to, device_id_type=MESH)
 
+    def rows_of(b):
+        return pl.ds(pl.multiple_of(b * block, block), block)
+
     def load(b):
-        at = pl.ds(b * block, block)
+        at = rows_of(b)
         return pltpu.make_async_copy(design_hbm.at[at], design.at[at], load_sem.at[b])
 
     for b in range(BLOCKS):
@@ -52,9 +61,6 @@
     lane = lax.broadcasted_iota(jnp.int32, (own, fits), 1)
     row = lax.broadcasted_iota(jnp.int32, (own, fits), 0)
     mine = (lane == row + own * r).astype(F32)
-
-    def rows_of(b):
-        return pl.ds(pl.multiple_of(b * block, block), block)
 
     def back_block(b, vectors):
         left = jnp.transpose(vectors).astype(BF16)
@@ -69,38 +75,60 @@
         def fits_of(i):
             return pl.ds(pl.multiple_of(i * own, own), own)
 
-        for j in range(chips):
-            cs[j] = h_ref[fits_of(2 * j + 1 - core), :].astype(BF16)
-        swap = remote(cs, cr, c_send, c_recv, (sibling, c))
-        swap.start()
-        swap.wait()
-
-        def send(d):
-            to = lax.rem(chip + d, chips)
-            return remote(rs.at[to], rr.at[chip], r_send.at[to], r_recv.at[chip], (2 * to + core, c))
-
-        def arrived(d):
-            frm = lax.rem(chip + d, chips)
-            return remote(rs.at[frm], rr.at[frm], r_send.at[frm], r_recv.at[frm], (2 * frm + core, c))
-
-        @pl.loop(1, chips)
-        def _(d):
-            to = lax.rem(chip + d, chips)
-            rs[to] = (h_ref[fits_of(2 * to + core), :] + cr[to].astype(F32)).astype(BF16)
-            send(d).start()
-
-        h_ref[fits_of(r), :] += cr[chip].astype(F32)
-
-        @pl.loop(1, chips)
-        def _(d):
-            arrived(d).wait_recv()
-            h_ref[fits_of(r), :] += rr[lax.rem(chip + d, chips)].astype(F32)
-
-        @pl.loop(1, chips)
-        def _(d):
-            send(d).wait_send()
-
-        return scale_ref[...] * h_ref[fits_of(r), :]
+        def swap(j):
+            return remote(cs.at[j], cr.at[j], c_send.at[j], c_recv.at[j], (sibling, c))
+
+        def cross(z):
+            return remote(ys.at[z], yr.at[z], y_send.at[z], y_recv.at[z], across)
+
+        def send(z):
+            return remote(rs.at[z], rr.at[place], r_send.at[z], r_recv.at[place],
+                          (4 * z + 2 * side + core, c))
+
+        def arrived(z):
+            return remote(rs.at[z], rr.at[z], r_send.at[z], r_recv.at[z],
+                          (4 * z + 2 * side + core, c))
+
+        def chip_sum(j):
+            swap(j).wait_recv()
+            return h_ref[fits_of(2 * j + core), :] + cr[j].astype(F32)
+
+        for other in (1 - side, side):
+            for d in order + [0]:
+                j = 2 * place_at(d) + other
+                cs[j] = h_ref[fits_of(2 * j + 1 - core), :].astype(BF16)
+                swap(j).start()
+
+        for d in order + [0]:
+            z = place_at(d)
+            ys[z] = chip_sum(2 * z + 1 - side).astype(BF16)
+            cross(z).start()
+
+        for d in order:
+            z = place_at(d)
+            part = chip_sum(2 * z + side)
+            cross(z).wait_recv()
+            rs[z] = (part + yr[z].astype(F32)).astype(BF16)
+            send(z).start()
+
+        total = chip_sum(chip)
+        cross(place).wait_recv()
+        total = total + yr[place].astype(F32)
+        for d in order:
+            z = place_at(line - d)
+            arrived(z).wait_recv()
+            total = total + rr[z].astype(F32)
+
+        @pl.loop(0, chips)
+        def _(j):
+            swap(j).wait_send()
+
+        for d in order + [0]:
+            cross(place_at(d)).wait_send()
+        for d in order:
+            send(place_at(d)).wait_send()
+
+        return scale_ref[...] * total
 
     def squared(g):
         gx[0] = jnp.broadcast_to(jnp.sum(g * g, axis=1, keepdims=True), (own, fits))
@@ -110,44 +138,50 @@
         return gx[0] + gx[1]
 
     def gather():
-        def send(d):
-            to = lax.rem(chip + d, chips)
-            return remote(sp_all.at[r], sp_all.at[r], a_send.at[to], a_recv.at[r], (2 * to + core, c))
-
-        def relay(d):
-            slot = 2 * lax.rem(chip + d, chips) + core
-            return remote(sp_all.at[slot], sp_all.at[slot], f_send.at[lax.div(slot, 2)],
-                          a_recv.at[slot], (sibling, c))
+        def send(z):
+            return remote(sp_all.at[r], sp_all.at[r], a_send.at[z], a_recv.at[r],
+                          (4 * z + 2 * side + core, c))
+
+        def cross(z):
+            slot = 4 * z + 2 * side + core
+            return remote(sp_all.at[slot], sp_all.at[slot], b_send.at[z], a_recv.at[slot], across)
+
+        def relay(j):
+            slot = 2 * j + core
+            return remote(sp_all.at[slot], sp_all.at[slot], f_send.at[j], a_recv.at[slot], (sibling, c))
 
         def arrived(slot):
-            return remote(sp_all.at[slot], sp_all.at[slot], a_send.at[0], a_recv.at[slot], (sibling, c))
-
-        @pl.loop(1, chips)
-        def _(d):
-            send(d).start()
-
-        relay(0).start()
-
-        @pl.loop(1, chips)
-        def _(d):
-            arrived(2 * lax.rem(chip + d, chips) + core).wait_recv()
-            relay(d).start()
+            return remote(sp_all.at[slot], sp_all.at[slot], f_send.at[0], a_recv.at[slot], (sibling, c))
+
+        cross(place).start()
+        for d in order:
+            send(place_at(d)).start()
+        relay(chip).start()
+        later = [line - d for d in reversed(order)]
+        for d in later:
+            z = place_at(d)
+            arrived(4 * z + 2 * side + core).wait_recv()
+            cross(z).start()
+            relay(2 * z + side).start()
+        for d in [0] + later:
+            j = 2 * place_at(d) + 1 - side
+            arrived(2 * j + core).wait_recv()
+            relay(j).start()
+        for other in (side, 1 - side):
+            for d in [0] + later:
+                j = 2 * place_at(d) + other
+                arrived(2 * j + 1 - core).wait_recv()
+                pair = jnp.concatenate([sp_all[2 * j].astype(F32), sp_all[2 * j + 1].astype(F32)], axis=0)
+                spm[pl.ds(pl.multiple_of(2 * own * j, 2 * own), 2 * own), :] = pair.astype(BF16)
+
+        for d in order:
+            send(place_at(d)).wait_send()
+        for d in [0] + later:
+            cross(place_at(d)).wait_send()
 
         @pl.loop(0, chips)
-        def _(d):
-            arrived(2 * lax.rem(chip + d, chips) + 1 - core).wait_recv()
-
-        for j in range(chips):
-            pair = jnp.concatenate([sp_all[2 * j].astype(F32), sp_all[2 * j + 1].astype(F32)], axis=0)
-            spm[2 * own * j:2 * own * (j + 1), :] = pair.astype(BF16)
-
-        @pl.loop(1, chips)
-        def _(d):
-            send(d).wait_send()
-
-        @pl.loop(0, chips)
-        def _(d):
-            relay(d).wait_send()
+        def _(j):
+            relay(j).wait_send()
 
     def x_copy(b):
         return remote(xs.at[b], xr.at[b], x_send.at[b], x_recv.at[b], partner)
@@ -207,11 +241,9 @@
     h_ref[...] = jnp.zeros_like(h_ref)
     res_ref[...] = targets_ref[...].astype(F32)
     sol_ref[...] = jnp.zeros_like(sol_ref)
-    for b in range(BLOCKS):
-        load(b).wait()
-
     @pl.loop(0, BLOCKS)
     def _(b):
+        load(b).wait()
         back_block(b, res_ref[rows_of(b), :])
 
     pl.semaphore_wait(barrier, n)
@@ -262,7 +294,7 @@
 def fused(n, design, targets, col_scale):
     rows, width = design.shape
     fits = targets.shape[1]
-    own, chips, block = fits // n, n // 2, rows // BLOCKS
+    own, chips, line, block = fits // n, n // 2, n // 4, rows // BLOCKS
     vmem = pl.BlockSpec(memory_space=pltpu.VMEM)
     dma = pltpu.SemaphoreType.DMA
     sol, res = pl.pallas_call(
@@ -281,15 +313,18 @@
             pltpu.VMEM((BLOCKS, block, fits), BF16),
             pltpu.VMEM((chips, own, width), BF16),
             pltpu.VMEM((chips, own, width), BF16),
-            pltpu.VMEM((chips, own, width), BF16),
-            pltpu.VMEM((chips, own, width), BF16),
+            pltpu.VMEM((line, own, width), BF16),
+            pltpu.VMEM((line, own, width), BF16),
+            pltpu.VMEM((line, own, width), BF16),
+            pltpu.VMEM((line, own, width), BF16),
             pltpu.VMEM((n, 2, fits), F32),
             pltpu.VMEM((2, own, fits), F32),
             pltpu.VMEM((own, width), F32),
             pltpu.VMEM((own, width), F32),
             pltpu.VMEM((own, fits), F32),
-            dma((BLOCKS,)), dma((BLOCKS,)), dma((BLOCKS,)), dma, dma,
-            dma((chips,)), dma((chips,)), dma((chips,)), dma((n,)), dma((chips,)),
+            dma((BLOCKS,)), dma((BLOCKS,)), dma((BLOCKS,)), dma((chips,)), dma((chips,)),
+            dma((line,)), dma((line,)), dma((line,)), dma((n,)), dma((line,)), dma((chips,)),
+            dma((line,)), dma((line,)),
             dma((n,)), dma((n,)), dma, dma,
         ],
         compiler_params=pltpu.CompilerParams(
@@ -342,7 +377,7 @@
         rows, width = design.shape
         fits = targets.shape[1]
         fits_tile = fits % (8 * n) == 0 and fits % 128 == 0
-        if pair == 2 and n % 2 == 0 and fits_tile and rows % (BLOCKS * 128) == 0 and width % 128 == 0:
+        if pair == 2 and n % 4 == 0 and fits_tile and rows % (BLOCKS * 128) == 0 and width % 128 == 0:
             return fused(n, design, targets, col_scale)
         return plain(design, targets, col_scale)
 

time: 271 us -> 258 us (0.952)
  Pallas kernels: 267 us -> 254 us
    pallas_call x1, Pallas kernels: 267 us -> 254 us  [fused(): pl.pallas_call(functools.partial(kernel, n), out_shape=(jax.ShapeDtypeStr...]
where the time goes in v2:
time: 258 us
  Pallas kernels  254 us (98%)
  local copies, waits for them, and re-layouts  3.35 us (1%)
    pallas_call x1, Pallas kernels, fused(): pl.pallas_call(functools.partial(kernel, n), out_shape=(jax.ShapeDtypeStr...  254 us

profile of v2, /device:TPU:0, one launch (start us, length us, event | category | flops | bytes accessed | tf_op | source)
XLA Modules:
  0.0 257.5 jit_solution(11814653844067699643)
XLA Ops:
  0.6 0.0 copy-start
  0.6 1.0 copy-done
  1.7 0.0 copy-start.1
  1.7 0.7 copy-done.1
  2.4 253.5 %cg.1 = (f32[8,3072]{1,0:T(8,128)S(1)}, f32[2048,128]{1,0:T(8,128)S(1)}) custom-call(bf16[2048,3072]{1,0:T(8,128)(2,1)} %design_hbm.1, bf16[2048,128]{1,0:T(8,128)(2,1)S(1)} %copy-done, f32[1,3072]{1,0:T(1,128)S(1)} %bitcast.3), custom_call_target="tpu_custom_call" | custom-call | tf_op jit(solution)/shard_map/cg/pallas_call | solution.py:300
  255.9 0.6 copy.7
  256.6 1.0 copy.8
Async XLA Ops:
  0.6 1.0 copy-start
  1.7 0.7 copy-start.1
